TPU v7x, 32 devices: a whole 2x2x4 slice. The times are simulated.
32 devices in a mesh: dp: 8 (over y, x, core), mp: 4 (over z).
Axes of the slice: x: 2, y: 2, z: 4, core: 2. Of those that a mesh axis runs over, the one named last changes fastest.
Arguments:
- candidates: bfloat16 [64, 256, 768], P('dp', 'mp'), may hold values from -6 to 6
- owner_row: int32 [64], replicated, may hold values from 0 to 63, as said below
- selected: int32 [16], replicated, may hold values from 0 to 63, as said below
- dest_slot: int32 [16], replicated, may hold values from 0 to 15, as said below
- patch_weight: bfloat16 [768, 768], P(None, 'mp'), may hold values from -0.21875 to 0.21875
- positions: bfloat16 [256, 768], P(None, 'mp'), may hold values from -3 to 3
- qkv_weight: bfloat16 [768, 3, 768], P(None, None, 'mp'), may hold values from -1 to 1
- out_weight: bfloat16 [768, 768], P('mp'), may hold values from -0.21875 to 0.21875
- attn_gain: bfloat16 [768], replicated, may hold values from 0.099609375 to 1.8984375
- mlp_gain: bfloat16 [768], replicated, may hold values from 0.099609375 to 1.8984375
- up_weight: bfloat16 [768, 3072], P(None, 'mp'), may hold values from -0.21875 to 0.21875
- down_weight: bfloat16 [3072, 768], P('mp'), may hold values from -0.109375 to 0.109375
Outputs:
- layer_out: bfloat16 [16, 256, 768], P('dp', 'mp')
Inputs may be any that keep to these rules, and one draw needn't show every extreme that they name: `owner_row`: a permutation; storage row r sits on index r // 8 of dp. `selected`: distinct candidates; no index of dp stores more than 4 of them, and some index stores exactly 4. `dest_slot`: a permutation; the 2 slots s with equal s // 2 get candidates stored on different indices of dp.
All inputs are finite; a program needn't handle non-finite values.
Results may differ from a plain program's by a relative error of at most 0.012.
Values may be sent and summed in bfloat16 or wider, within the bound.
No kernel may reach another device: no remote copies, remote signals or barrier semaphores. Data moves between devices by JAX's collectives and lax.ppermute only.
A program may use at most 128 MiB of HBM per device.

v0:
```python
import jax
import jax.numpy as jnp
from jax import lax
from jax.sharding import PartitionSpec as P

PATCHES = 256
CAND_DEV = 8
SEL_DEV = 2
HEAD_DIM = 64


def norm_rows(values, gain):
    average = jnp.mean(values, axis=-1, keepdims=True)
    centred = values - average
    variance = jnp.mean(centred * centred, axis=-1, keepdims=True)
    return centred * lax.rsqrt(variance + 1e-06) * gain.astype(jnp.float32)


def local(
    candidates,
    owner_row,
    selected,
    dest_slot,
    patch_weight,
    positions,
    qkv_weight,
    out_weight,
    attn_gain,
    mlp_gain,
    up_weight,
    down_weight,
):
    learners = lax.axis_size("dp")
    own_index = lax.axis_index("dp")
    quarter = candidates.shape[1]
    pixel_width = candidates.shape[2]
    chosen_rows = jnp.take(owner_row, selected)
    slot_rows = jnp.zeros(dest_slot.shape, jnp.int32).at[dest_slot].set(chosen_rows)
    source_owner = slot_rows // CAND_DEV
    local_row = slot_rows % CAND_DEV
    stored = candidates.reshape(CAND_DEV, quarter * pixel_width)
    mine = (source_owner == own_index).reshape(learners, SEL_DEV)
    picked = jnp.sum(jnp.where(mine, local_row.reshape(learners, SEL_DEV), 0), axis=1)
    outgoing = jnp.take(stored, picked, axis=0)
    incoming = lax.all_to_all(outgoing, "dp", split_axis=0, concat_axis=0, tiled=True)
    senders = lax.dynamic_slice_in_dim(source_owner, own_index * SEL_DEV, SEL_DEV)
    arrived = jnp.take(incoming, senders, axis=0)
    own_pixels = arrived.reshape(SEL_DEV, quarter, pixel_width)
    product = jnp.einsum(
        "brp,pe->bre",
        lax.all_gather(own_pixels, "mp", axis=1, tiled=True),
        patch_weight,
        preferred_element_type=jnp.float32,
    )
    embedded = (product + positions.astype(jnp.float32)[None]).astype(jnp.bfloat16)
    activations = lax.all_gather(embedded, "mp", axis=2, tiled=True).astype(jnp.float32)
    normed = norm_rows(activations, attn_gain).astype(jnp.bfloat16)
    projected = jnp.einsum(
        "btd,dce->btce", normed, qkv_weight, preferred_element_type=jnp.float32
    ).astype(jnp.bfloat16)
    local_heads = qkv_weight.shape[2] // HEAD_DIM
    head_split = projected.reshape(SEL_DEV, PATCHES, 3, local_heads, HEAD_DIM)
    queries = head_split[:, :, 0]
    attn_keys = head_split[:, :, 1]
    attn_values = head_split[:, :, 2]
    scores = jnp.einsum(
        "bqhd,bkhd->bhqk", queries, attn_keys, preferred_element_type=jnp.float32
    ) * HEAD_DIM ** (-0.5)
    attn_probs = jax.nn.softmax(scores, axis=-1).astype(jnp.bfloat16)
    context = jnp.einsum(
        "bhqk,bkhd->bqhd", attn_probs, attn_values, preferred_element_type=jnp.float32
    ).astype(jnp.bfloat16)
    context = context.reshape(SEL_DEV, PATCHES, local_heads * HEAD_DIM)
    partial_out = jnp.einsum("bte,ed->btd", context, out_weight, preferred_element_type=jnp.float32)
    attended = lax.psum(partial_out.astype(jnp.bfloat16), "mp").astype(jnp.float32)
    after_attn = activations + attended
    normed2 = norm_rows(after_attn, mlp_gain).astype(jnp.bfloat16)
    hidden = jax.nn.gelu(
        jnp.einsum("btd,df->btf", normed2, up_weight, preferred_element_type=jnp.float32),
        approximate=False,
    ).astype(jnp.bfloat16)
    down_terms = jnp.einsum("btf,fd->btd", hidden, down_weight, preferred_element_type=jnp.float32)
    summed = lax.psum_scatter(
        down_terms.astype(jnp.bfloat16), "mp", scatter_dimension=1, tiled=True
    ).astype(jnp.float32)
    residual = lax.dynamic_slice_in_dim(after_attn, lax.axis_index("mp") * quarter, quarter, 1)
    return (residual + summed).astype(jnp.bfloat16)


def solution(mesh):
    return jax.shard_map(
        local,
        mesh=mesh,
        in_specs=(
            P("dp", "mp", None),
            P(),
            P(),
            P(),
            P(None, "mp"),
            P(None, "mp"),
            P(None, None, "mp"),
            P("mp", None),
            P(),
            P(),
            P(None, "mp"),
            P("mp", None),
        ),
        out_specs=P("dp", "mp", None),
        check_vma=False,
    )
```

profile of v0, /device:TPU:0, one launch (start us, length us, event | category | flops | bytes accessed | tf_op | source)
XLA Modules:
  0.0 183.8 jit_solution(13271876456663978697)
XLA Ops:
  6.5 0.8 compare_select_fusion.3
  7.3 1.3 gather_fusion
  8.6 0.7 compare_select_fusion.4
  9.3 0.6 scatter_custom_fusion
  10.2 1.6 copy.77
  11.8 1.1 gather_fusion.1
  13.0 0.5 broadcast.218
  13.5 1.2 reduce.4
  14.7 1.5 reshape.149
  16.2 5.2 %all-to-all-start = ((bf16[8,2,24576]{2,1,0:T(2,128)(2,1)}), bf16[8,2,24576]{2,1,0:T(2,128)(2,1)S(1)}, u32[]{:S(2)}, u32[]{:S(2)}) async-start(bf16[8,2,24576]{2,1,0:T(2,128)(2,1)} %reshape.149), calls=%async_computation | async-start | bytes 1572864 | tf_op jit(solution)/shard_map/all_to_all | solution.py:45
  21.5 0.7 convert_element_type.51
  22.3 11.7 %all-to-all-done = bf16[8,2,24576]{2,1,0:T(2,128)(2,1)S(1)} async-done(((bf16[8,2,24576]{2,1,0:T(2,128)(2,1)}), bf16[8,2,24576]{2,1,0:T(2,128)(2,1)S(1)}, u32[]{:S(2)}, u32[]{:S(2)}) %all-to-all-start) | async-done | bytes 786464 | tf_op jit(solution)/shard_map/all_to_all | solution.py:45
  34.0 0.8 reshape.150
  34.8 0.9 copy.82
  35.7 0.8 gather_fusion.2
  36.6 18.1 %all_gather.6 = bf16[2,256,768]{2,1,0:T(8,128)(2,1)S(1)} all-gather(bf16[2,64,768]{2,1,0:T(8,128)(2,1)S(1)} %bitcast_select_fusion.1), channel_id=1, replica_groups=mesh['dp'=8,'mp'=4] {'mp'}, dimensions={1}, use_global_device_ids=true | all-gather | bytes 983040 | tf_op jit(solution)/shard_map/all_gather | solution.py:51
  55.3 17.4 %all_gather.7 = bf16[2,256,768]{1,0,2:T(2,128)(2,1)S(1)} all-gather(bf16[2,256,192]{1,0,2:T(2,128)(2,1)S(1)} %copy.63), channel_id=1, replica_groups=mesh['dp'=8,'mp'=4] {'mp'}, dimensions={2}, use_global_device_ids=true | all-gather | bytes 983040 | tf_op jit(solution)/shard_map/all_gather | solution.py:56
  72.7 0.6 copy.64
  73.9 0.6 copy-done.9
  74.5 0.8 convolution_convert_fusion.2
  75.3 0.7 fusion.108
  76.0 0.9 convolution_convert_fusion.3
  76.9 1.3 convolution_convert_fusion.1
  78.5 44.0 %all-reduce.4.cloned.1.call-done = bf16[2,256,768]{2,1,0:T(8,128)(2,1)} async-done(((bf16[2,256,768]{2,1,0:T(8,128)(2,1)}), bf16[2,256,768]{2,1,0:T(8,128)(2,1)}) %all-reduce.4.cloned.1.call-update) | async-done | bytes 786448 | tf_op jit(solution)/shard_map/psum | solution.py:75
  122.5 1.5 fusion.107
  124.5 1.3 fusion.63
  125.7 4.4 %convolution_convert_fusion = bf16[2,256,768]{2,1,0:T(8,128)(2,1)S(1)} fusion(bf16[768,768]{1,0:T(8,128)(2,1)S(1)} %copy-done.8, f32[2,256,768]{2,1,0:T(8,128)S(1)} %get-tuple-element.13, u8[256,768]{1,0:T(8,128)(4,1)S(1)} %get-tuple-element.6, u8[256,768]{1,0:T(8,128)(4,1)S(1)} %get-tuple-element.5), kind=kOutput, calls=%fused_computation.41 | convolution fusion | flops 631898112 | bytes 3932160 | tf_op jit(solution)/shard_map/btf,fd->btd/dot_general | solution.py:82
  130.2 1.7 copy.69
  131.9 0.6 dynamic-slice
  133.2 42.0 %all-reduce.6.cloned.1.call-done = bf16[2,256,768]{2,0,1:T(2,128)(2,1)} async-done(((bf16[2,256,768]{2,0,1:T(2,128)(2,1)}), bf16[2,256,768]{2,0,1:T(2,128)(2,1)}) %all-reduce.6.cloned.1.call-update) | async-done | bytes 786448
  175.2 1.1 constant_dynamic-slice_fusion
  176.3 0.7 add_convert_fusion
  (47 shorter events, 2.6 us)
Async XLA Ops:
  6.5 117.9 %copy-start = (bf16[768,768]{1,0:T(8,128)(2,1)S(1)}, bf16[768,768]{1,0:T(8,128)(2,1)}, u32[]{:S(2)}) copy-start(bf16[768,768]{1,0:T(8,128)(2,1)} %param.22) | copy-start | bytes 3538948
  14.7 6.8 %copy-start.5 = (bf16[256,192]{0,1:T(8,128)(2,1)S(1)}, bf16[256,192]{0,1:T(8,128)(2,1)}, u32[]{:S(2)}) copy-start(bf16[256,192]{0,1:T(8,128)(2,1)} %param.17) | copy-start | bytes 294916
  14.7 7.5 %copy-start.6 = (bf16[768]{0:T(1024)(128)(2,1)S(1)}, bf16[768]{0:T(1024)(128)(2,1)}, u32[]{:S(2)}) copy-start(bf16[768]{0:T(1024)(128)(2,1)} %param.20) | copy-start | bytes 4612
  16.2 17.8 %all-to-all-start = ((bf16[8,2,24576]{2,1,0:T(2,128)(2,1)}), bf16[8,2,24576]{2,1,0:T(2,128)(2,1)S(1)}, u32[]{:S(2)}, u32[]{:S(2)}) async-start(bf16[8,2,24576]{2,1,0:T(2,128)(2,1)} %reshape.149), calls=%async_computation | async-start | bytes 1572864 | tf_op jit(solution)/shard_map/all_to_all | solution.py:45
  21.4 101.1 %all-reduce.4.cloned.1.call-start = ((), (), s32[]{:S(2)}) async-start(), calls=%async_computation.1 | async-start | bytes 1572864 | tf_op jit(solution)/shard_map/psum | solution.py:75
  35.7 19.0 %copy-start.2 = (f32[256,192]{0,1:T(8,128)S(1)}, f32[256,192]{0,1:T(8,128)}, u32[]{:S(2)}) copy-start(f32[256,192]{0,1:T(8,128)} %convert_element_type.51) | copy-start | bytes 589828
  35.7 19.0 %copy-start.4 = (bf16[768,192]{0,1:T(8,128)(2,1)S(1)}, bf16[768,192]{0,1:T(8,128)(2,1)}, u32[]{:S(2)}) copy-start(bf16[768,192]{0,1:T(8,128)(2,1)} %param.16) | copy-start | bytes 884740
  73.3 1.2 copy-start.9
  76.0 1.0 copy-start.3
  76.9 1.6 copy-start.7
  78.3 96.9 %all-reduce.6.cloned.1.call-start = ((), (), s32[]{:S(2)}) async-start(), calls=%async_computation.2 | async-start | bytes 1572864
  122.5 1.5 copy-start.1
  124.4 1.3 copy-start.8
  130.2 1.8 copy-start.10
Sparse Core Ops, SparseCore 0:
  78.4 44.0 all-reduce.3
  132.0 43.1 all-reduce.5
where the time goes:
time: 184 us
  waiting for transfers between devices  97.8 us (53%)
  blocking collectives  35.5 us (19%)
  between operations  14.3 us (8%)
  local copies, waits for them, and re-layouts  14 us (8%)
  matrix products  9.79 us (5%)
  other arithmetic  7.02 us (4%)
  starting transfers between devices  5.46 us (3%)
    psum x1, waiting for transfers between devices, local(): lax.psum(partial_out.astype(jnp.bfloat16), 'mp').astype(jnp.float32)  44 us
    unnamed x3, waiting for transfers between devices  42.1 us
    all_gather x1, blocking collectives, local(): lax.all_gather(own_pixels, 'mp', axis=1, tiled=True)  18.1 us
    all_gather x1, blocking collectives, local(): lax.all_gather(embedded, 'mp', axis=2, tiled=True).astype(jnp.float32)  17.4 us
    all_to_all x1, waiting for transfers between devices, local(): lax.all_to_all(outgoing, 'dp', split_axis=0, concat_axis=0, tiled=True)  11.7 us
    unnamed x28, local copies, waits for them, and re-layouts  7.11 us
    all_to_all x1, starting transfers between devices, local(): lax.all_to_all(outgoing, 'dp', split_axis=0, concat_axis=0, tiled=True)  5.2 us
    dot_general x1, matrix products, local(): jnp.einsum('btf,fd->btd', hidden, down_weight, preferred_element_type=jnp...  4.43 us
  transfers between devices with their start and end apart: 3, of which 3 were waited for; matrix products, arithmetic and copies ran while one was open for 1% of the time, Pallas kernels for 0%

commit v1 on v0

--- a/solution.py
+++ b/solution.py
@@ -53,7 +53,7 @@
         preferred_element_type=jnp.float32,
     )
     embedded = (product + positions.astype(jnp.float32)[None]).astype(jnp.bfloat16)
-    activations = lax.all_gather(embedded, "mp", axis=2, tiled=True).astype(jnp.float32)
+    activations = jnp.concatenate(lax.all_gather(embedded, "mp"), axis=2).astype(jnp.float32)
     normed = norm_rows(activations, attn_gain).astype(jnp.bfloat16)
     projected = jnp.einsum(
         "btd,dce->btce", normed, qkv_weight, preferred_element_type=jnp.float32

time: 184 us -> 165 us (0.90)
  waiting for transfers between devices: 97.8 us -> 76.6 us
  matrix products: 9.79 us -> 13.2 us
  local copies, waits for them, and re-layouts: 14 us -> 12.1 us
    unnamed x3 -> x2, waiting for transfers between devices: 42.1 us -> 0.03 us
    reduce_scatter x0 -> x1, waiting for transfers between devices: none -> 22.6 us  [local(): lax.psum_scatter(down_terms.astype(jnp.bfloat16), 'mp', scatter_dimension...]
    unnamed x28 -> x22, local copies, waits for them, and re-layouts: 7.11 us -> 5.99 us
where the time goes in v1:
time: 165 us
  waiting for transfers between devices  76.6 us (46%)
  blocking collectives  35.6 us (22%)
  between operations  13.7 us (8%)
  matrix products  13.2 us (8%)
  local copies, waits for them, and re-layouts  12.1 us (7%)
  other arithmetic  8.16 us (5%)
  starting transfers between devices  5.28 us (3%)
    psum x1, waiting for transfers between devices, local(): lax.psum(partial_out.astype(jnp.bfloat16), 'mp').astype(jnp.float32)  42.3 us
    reduce_scatter x1, waiting for transfers between devices, local(): lax.psum_scatter(down_terms.astype(jnp.bfloat16), 'mp', scatter_dimension...  22.6 us
    all_gather x1, blocking collectives, local(): lax.all_gather(own_pixels, 'mp', axis=1, tiled=True)  18.1 us
    all_gather x1, blocking collectives, local(): lax.all_gather(embedded, 'mp')  17.6 us
    all_to_all x1, waiting for transfers between devices, local(): lax.all_to_all(outgoing, 'dp', split_axis=0, concat_axis=0, tiled=True)  11.7 us
    unnamed x22, local copies, waits for them, and re-layouts  5.99 us
    all_to_all x1, starting transfers between devices, local(): lax.all_to_all(outgoing, 'dp', split_axis=0, concat_axis=0, tiled=True)  5.2 us
    dot_general x1, matrix products, local(): jnp.einsum('btf,fd->btd', hidden, down_weight, preferred_element_type=jnp...  5.16 us
  transfers between devices with their start and end apart: 3, of which 3 were waited for; matrix products, arithmetic and copies ran while one was open for 1% of the time, Pallas kernels for 0%

profile of v1, /device:TPU:0, one launch (start us, length us, event | category | flops | bytes accessed | tf_op | source)
XLA Modules:
  0.0 164.7 jit_solution(15594938857447014045)
XLA Ops:
  6.5 0.8 compare_select_fusion.3
  7.3 1.3 gather_fusion
  8.6 0.7 compare_select_fusion.4
  9.3 0.6 scatter_custom_fusion
  10.2 1.6 copy.48
  11.8 1.1 gather_fusion.1
  13.0 0.5 broadcast.219
  13.5 1.2 reduce.6
  14.7 1.5 reshape.156
  16.2 5.2 %all-to-all-start = ((bf16[8,2,24576]{2,1,0:T(2,128)(2,1)}), bf16[8,2,24576]{2,1,0:T(2,128)(2,1)S(1)}, u32[]{:S(2)}, u32[]{:S(2)}) async-start(bf16[8,2,24576]{2,1,0:T(2,128)(2,1)} %reshape.156), calls=%async_computation | async-start | bytes 1572864 | tf_op jit(solution)/shard_map/all_to_all | solution.py:45
  21.5 0.7 convert_element_type.62
  22.3 11.7 %all-to-all-done = bf16[8,2,24576]{2,1,0:T(2,128)(2,1)S(1)} async-done(((bf16[8,2,24576]{2,1,0:T(2,128)(2,1)}), bf16[8,2,24576]{2,1,0:T(2,128)(2,1)S(1)}, u32[]{:S(2)}, u32[]{:S(2)}) %all-to-all-start) | async-done | bytes 786464 | tf_op jit(solution)/shard_map/all_to_all | solution.py:45
  34.0 0.8 reshape.157
  34.8 0.9 copy.52
  35.7 0.8 gather_fusion.2
  36.6 18.1 %all_gather.9 = bf16[2,256,768]{2,1,0:T(8,128)(2,1)S(1)} all-gather(bf16[2,64,768]{2,1,0:T(8,128)(2,1)S(1)} %bitcast_select_fusion.1), channel_id=1, replica_groups=mesh['dp'=8,'mp'=4] {'mp'}, dimensions={1}, use_global_device_ids=true | all-gather | bytes 983040 | tf_op jit(solution)/shard_map/all_gather | solution.py:51
  54.7 0.4 fusion.15
  55.1 17.6 %all-gather = bf16[8,256,192]{1,2,0:T(8,128)(2,1)S(1)} all-gather(bf16[2,256,192]{1,2,0:T(8,128)(2,1)S(1)} %fusion.15), channel_id=2, replica_groups=mesh['dp'=8,'mp'=4] {'mp'}, dimensions={0}, use_global_device_ids=true | all-gather | bytes 983040 | tf_op jit(solution)/shard_map/all_gather | solution.py:56
  73.0 0.2 multiply_reduce_fusion.1
  73.3 1.0 copy-done.8
  74.4 1.5 convolution_convert_fusion.2
  75.9 1.7 %fusion.104 = f32[2,3,256]{2,1,0:T(4,128)S(1)} fusion(bf16[2,256,3,3,64]{1,4,3,2,0:T(8,128)(2,1)} %bitcast.10), kind=kOutput, calls=%fused_computation.159 | convolution fusion | flops 51511552 | bytes 399360 | tf_op jit(solution)/shard_map/sub | solution.py:69
  77.6 2.0 %convolution_convert_fusion.3 = bf16[2,3,64,256]{3,2,1,0:T(8,128)(2,1)S(1)} fusion(f32[2,3,256]{2,1,0:T(4,128)S(1)} %fusion.104, bf16[2,256,3,3,64]{1,4,3,2,0:T(8,128)(2,1)} %bitcast.10), kind=kOutput, calls=%fused_computation.45 | convolution fusion | flops 102336256 | bytes 792576 | tf_op jit(solution)/shard_map/bhqk,bkhd->bqhd/dot_general | solution.py:70
  79.7 1.3 convolution_convert_fusion.1
  81.1 1.6 copy.39
  82.7 42.3 %all-reduce.2.cloned.1.call-done = bf16[2,256,768]{2,1,0:T(8,128)(2,1)} async-done(((bf16[2,256,768]{2,1,0:T(8,128)(2,1)}), bf16[2,256,768]{2,1,0:T(8,128)(2,1)}) %all-reduce.2.cloned.1.call-update) | async-done | bytes 786448 | tf_op jit(solution)/shard_map/psum | solution.py:75
  125.0 1.8 %fusion.103 = (f32[2,256]{1,0:T(2,128)S(1)}, f32[2,256,768]{2,1,0:T(8,128)S(1)}) fusion(f32[2,256,768]{2,1,0:T(8,128)} %copy.39, bf16[2,256,768]{2,1,0:T(8,128)(2,1)} %all-reduce.2.cloned.1.call-done), kind=kLoop, calls=%fused_computation.158 | loop fusion | flops 1179136 | bytes 3934208 | tf_op jit(solution)/shard_map/reduce_sum | solution.py:13
  126.9 0.3 multiply_reduce_fusion
  127.2 1.1 fusion.59
  128.5 5.2 %convolution_convert_fusion = bf16[2,256,768]{2,1,0:T(8,128)(2,1)} fusion(bf16[768,768]{1,0:T(8,128)(2,1)S(1)} %copy-done.7, f32[2,256,768]{2,1,0:T(8,128)S(1)} %get-tuple-element.13, u8[256,768]{1,0:T(8,128)(4,1)S(1)} %get-tuple-element.6, u8[256,768]{1,0:T(8,128)(4,1)S(1)} %get-tuple-element.5), kind=kOutput, calls=%fused_computation.37 | convolution fusion | flops 631898112 | bytes 3932160 | tf_op jit(solution)/shard_map/btf,fd->btd/dot_general | solution.py:82
  133.7 22.6 %reduce-scatter.2.cloned.1.call-done = bf16[2,64,768]{2,1,0:T(8,128)(2,1)} async-done(((bf16[2,256,768]{2,1,0:T(8,128)(2,1)}), bf16[2,64,768]{2,1,0:T(8,128)(2,1)}) %reduce-scatter.2.cloned.1.call-update) | async-done | bytes 196624 | tf_op jit(solution)/shard_map/reduce_scatter | solution.py:83
  156.2 1.6 add_convert_fusion
  (41 shorter events, 1.3 us)
Async XLA Ops:
  6.5 120.7 %copy-start = (bf16[768,768]{1,0:T(8,128)(2,1)S(1)}, bf16[768,768]{1,0:T(8,128)(2,1)}, u32[]{:S(2)}) copy-start(bf16[768,768]{1,0:T(8,128)(2,1)} %param.22) | copy-start | bytes 3538948
  14.7 6.8 %copy-start.5 = (bf16[768]{0:T(1024)(128)(2,1)S(1)}, bf16[768]{0:T(1024)(128)(2,1)}, u32[]{:S(2)}) copy-start(bf16[768]{0:T(1024)(128)(2,1)} %param.20) | copy-start | bytes 4612
  14.7 6.8 %copy-start.4 = (bf16[256,192]{0,1:T(8,128)(2,1)S(1)}, bf16[256,192]{0,1:T(8,128)(2,1)}, u32[]{:S(2)}) copy-start(bf16[256,192]{0,1:T(8,128)(2,1)} %param.17) | copy-start | bytes 294916
  16.2 17.8 %all-to-all-start = ((bf16[8,2,24576]{2,1,0:T(2,128)(2,1)}), bf16[8,2,24576]{2,1,0:T(2,128)(2,1)S(1)}, u32[]{:S(2)}, u32[]{:S(2)}) async-start(bf16[8,2,24576]{2,1,0:T(2,128)(2,1)} %reshape.156), calls=%async_computation | async-start | bytes 1572864 | tf_op jit(solution)/shard_map/all_to_all | solution.py:45
  21.4 103.6 %all-reduce.2.cloned.1.call-start = ((), (), s32[]{:S(2)}) async-start(), calls=%async_computation.2 | async-start | bytes 1572864 | tf_op jit(solution)/shard_map/psum | solution.py:75
  35.7 19.0 %copy-start.1 = (f32[256,192]{0,1:T(8,128)S(1)}, f32[256,192]{0,1:T(8,128)}, u32[]{:S(2)}) copy-start(f32[256,192]{0,1:T(8,128)} %convert_element_type.62) | copy-start | bytes 589828
  35.7 19.0 %copy-start.3 = (bf16[768,192]{0,1:T(8,128)(2,1)S(1)}, bf16[768,192]{0,1:T(8,128)(2,1)}, u32[]{:S(2)}) copy-start(bf16[768,192]{0,1:T(8,128)(2,1)} %param.16) | copy-start | bytes 884740
  73.2 1.2 copy-start.8
  77.6 2.1 %copy-start.2 = (bf16[192,768]{1,0:T(8,128)(2,1)S(1)}, bf16[192,768]{1,0:T(8,128)(2,1)}, u32[]{:S(2)}) copy-start(bf16[192,768]{1,0:T(8,128)(2,1)} %param.19) | copy-start | bytes 884740
  79.6 1.4 copy-start.6
  81.0 75.2 %reduce-scatter.2.cloned.1.call-start = ((), (), s32[]{:S(2)}) async-start(), calls=%async_computation.3 | async-start | bytes 983040 | tf_op jit(solution)/shard_map/reduce_scatter | solution.py:83
  127.2 1.3 copy-start.7
Sparse Core Ops, SparseCore 0:
  81.1 43.8 all-reduce.1
  133.8 22.3 reduce-scatter.1
